TPU v7x, 32 devices: a whole 2x2x4 slice. The times are simulated.
32 devices in a mesh: south: 2 (over x), east: 4 (over y, core), down: 4 (over z).
Axes of the slice: x: 2, y: 2, z: 4, core: 2. Of those that a mesh axis runs over, the one named last changes fastest.
Arguments:
- field_values: float32 [256, 32, 32, 128], P('south', 'east', 'down'), may hold values from 0.5 to 2
- flow_j: float32 [256, 32, 32, 128], P('south', 'east', 'down'), may hold values from -0.3 to 0.3
- flow_i: float32 [256, 32, 32, 128], P('south', 'east', 'down'), may hold values from -0.3 to 0.3
- flow_k: float32 [256, 32, 32, 128], P('south', 'east', 'down'), may hold values from -0.3 to 0.3
Outputs:
- standardized: float32 [256, 32, 32, 128], P('south', 'east', 'down')
- field_values_end: float32 [256, 32, 32, 128], P('south', 'east', 'down')
All inputs are finite; a program needn't handle non-finite values.
Results may differ from a plain program's by a relative error of at most 0.00002.
Values sent between devices are 32-bit elements; how exact they have to be, the bound alone decides.
A program may use at most 128 MiB of HBM per device.

v0:
```python
import jax
import jax.numpy as jnp
from jax import lax
from jax.sharding import PartitionSpec as P

STEPS = 6


def extended(block, sides, width):
    for axis, dim in sides:
        count = lax.axis_size(axis)
        forward = [(i, i + 1) for i in range(count - 1)]
        backward = [(target, source) for source, target in forward]
        low = lax.ppermute(
            lax.slice_in_dim(block, block.shape[dim] - width, None, axis=dim), axis, forward
        )
        high = lax.ppermute(lax.slice_in_dim(block, 0, width, axis=dim), axis, backward)
        block = jnp.concatenate([low, block, high], axis=dim)
    return block


def inner_cells(values, dims):
    for dim in dims:
        values = lax.slice_in_dim(values, 1, values.shape[dim] - 1, axis=dim)
    return values


def side_cells(values, dim, start, dims):
    others = [other for other in dims if other != dim]
    values = inner_cells(values, others)
    return lax.slice_in_dim(values, start, start + values.shape[dim] - 2, axis=dim)


def advance(padded, flow_j, flow_i, flow_k):
    middle = inner_cells(padded, (0, 1, 2))
    lower = [side_cells(padded, dim, 0, (0, 1, 2)) for dim in (0, 1, 2)]
    upper = [side_cells(padded, dim, 2, (0, 1, 2)) for dim in (0, 1, 2)]
    slopes = [above - below for above, below in zip(upper, lower)]
    smooth_rate = 0.05
    spread = lower[0] + upper[0] + lower[1] + upper[1] + lower[2] + upper[2] - 6.0 * middle
    return (
        middle - flow_j * slopes[0] - flow_i * slopes[1] - flow_k * slopes[2] + smooth_rate * spread
    )


def per_device(field_values, flow_j, flow_i, flow_k):
    for step in range(STEPS):
        padded = extended(field_values, (("south", 0), ("east", 1), ("down", 2)), 1)
        field_values = advance(padded, flow_j, flow_i, flow_k)
    count = field_values.shape[0] * lax.axis_size("south")
    line_mean = lax.psum(jnp.sum(field_values, axis=0, keepdims=True), "south") / count
    centred = field_values - line_mean
    line_variance = lax.psum(jnp.sum(centred * centred, axis=0, keepdims=True), "south") / count
    standardized = centred * lax.rsqrt(line_variance + 0.0001)
    return (standardized, field_values)


def solution(mesh):
    return jax.shard_map(
        per_device,
        mesh=mesh,
        in_specs=(
            P("south", "east", "down", None),
            P("south", "east", "down", None),
            P("south", "east", "down", None),
            P("south", "east", "down", None),
        ),
        out_specs=(P("south", "east", "down", None), P("south", "east", "down", None)),
        check_vma=False,
    )
```

profile of v0, /device:TPU:0, one launch (start us, length us, event | category | flops | bytes accessed | tf_op | source)
XLA Modules:
  0.0 316.3 jit_solution(3366898619759669091)
XLA Ops:
  1.4 4.9 %collective-permute-start.1 = (f32[1,8,8,128]{3,2,1,0:T(8,128)S(1)}, f32[1,8,8,128]{3,2,1,0:T(8,128)S(1)}, u32[]{:S(2)}, u32[]{:S(2)}) collective-permute-start(f32[1,8,8,128]{3,2,1,0:T(8,128)S(1)} %get-tuple-element.41), channel_id=1, source_target_pairs={{0,16},{1,17},{2,18},{3,19},{4,20},{5,21},{6,22},{7,23},{8,24},{9,... | collective-permute-start | bytes 98312 | tf_op jit(solution)/shard_map/ppermute | solution.py:14
  22.1 4.6 %collective-permute-start.5 = (f32[130,10,1,128]{3,0,2,1:T(8,128)S(1)}, f32[130,10,1,128]{3,0,2,1:T(8,128)S(1)}, u32[]{:S(2)}, u32[]{:S(2)}) collective-permute-start(f32[130,10,1,128]{3,0,2,1:T(8,128)S(1)} %copy.35), channel_id=1, source_target_pairs={{0,1},{1,2},{2,3},{4,5},{5,6},{6,7},{8,9},{9,10},{10,11},{12,13},{... | collective-permute-start | bytes 1996808 | tf_op jit(solution)/shard_map/ppermute | solution.py:14
  26.7 7.8 %collective-permute-done.4 = f32[130,10,1,128]{3,0,2,1:T(8,128)S(1)} collective-permute-done((f32[130,10,1,128]{3,0,2,1:T(8,128)S(1)}, f32[130,10,1,128]{3,0,2,1:T(8,128)S(1)}, u32[]{:S(2)}, u32[]{:S(2)}) %collective-permute-start.4) | collective-permute-done | bytes 665632 | tf_op jit(solution)/shard_map/ppermute | solution.py:17
  37.1 11.6 %multiply_add_fusion.5 = f32[128,8,8,128]{3,2,1,0:T(8,128)S(1)} fusion(f32[128,8,8,128]{3,2,1,0:T(8,128)S(1)} %copy-done.6, f32[128,8,8,128]{3,2,1,0:T(8,128)S(1)} %copy-done, f32[130,10,1,128]{3,2,1,0:T(1,128)S(1)} %copy.34, f32[130,1,8,128]{3,2,1,0:T(8,128)} %copy-done.12, f32[130,8,8,128]{3,2,1,0:T(8,128)} %copy-done.5, f32[130,1,8,128]{3,2,1,0:T(8,128)} %copy-done.7, ...), kind=kLoop, calls=%fused_computation.106 | loop fusion | flops 29360128 | bytes 27693056 | tf_op jit(solution)/shard_map/add | solution.py:42
  53.0 4.2 %collective-permute-done.6 = f32[1,8,8,128]{3,2,1,0:T(8,128)S(1)} collective-permute-done((f32[1,8,8,128]{3,2,1,0:T(8,128)S(1)}, f32[1,8,8,128]{3,2,1,0:T(8,128)S(1)}, u32[]{:S(2)}, u32[]{:S(2)}) %collective-permute-start.6) | collective-permute-done | bytes 32800 | tf_op jit(solution)/shard_map/ppermute | solution.py:17
  57.4 6.9 %collective-permute-start.9 = (f32[130,1,8,128]{3,2,1,0:T(8,128)S(1)}, f32[130,1,8,128]{3,2,1,0:T(8,128)S(1)}, u32[]{:S(2)}, u32[]{:S(2)}) collective-permute-start(f32[130,1,8,128]{3,2,1,0:T(8,128)S(1)} %get-tuple-element.26), channel_id=1, source_target_pairs={{0,4},{4,8},{8,12},{1,5},{5,9},{9,13},{2,6},{6,10},{10,14},{3,7},{... | collective-permute-start | bytes 1597448 | tf_op jit(solution)/shard_map/ppermute | solution.py:14
  71.6 5.1 %collective-permute-start.11 = (f32[130,10,1,128]{3,0,2,1:T(8,128)S(1)}, f32[130,10,1,128]{3,0,2,1:T(8,128)S(1)}, u32[]{:S(2)}, u32[]{:S(2)}) collective-permute-start(f32[130,10,1,128]{3,0,2,1:T(8,128)S(1)} %copy.39), channel_id=1, source_target_pairs={{0,1},{1,2},{2,3},{4,5},{5,6},{6,7},{8,9},{9,10},{10,11},{12,13},{... | collective-permute-start | bytes 1996808 | tf_op jit(solution)/shard_map/ppermute | solution.py:14
  76.7 7.5 %collective-permute-done.10 = f32[130,10,1,128]{3,0,2,1:T(8,128)S(1)} collective-permute-done((f32[130,10,1,128]{3,0,2,1:T(8,128)S(1)}, f32[130,10,1,128]{3,0,2,1:T(8,128)S(1)}, u32[]{:S(2)}, u32[]{:S(2)}) %collective-permute-start.10) | collective-permute-done | bytes 665632 | tf_op jit(solution)/shard_map/ppermute | solution.py:17
  86.7 10.8 %multiply_add_fusion.4 = f32[128,8,8,128]{3,2,1,0:T(8,128)S(1)} fusion(f32[128,8,8,128]{3,2,1,0:T(8,128)S(1)} %multiply_add_fusion.5, f32[128,8,8,128]{3,2,1,0:T(8,128)S(1)} %copy-done, f32[130,10,1,128]{3,2,1,0:T(1,128)S(1)} %copy.38, f32[130,1,8,128]{3,2,1,0:T(8,128)} %copy-done.13, f32[1,8,8,128]{3,2,1,0:T(8,128)S(1)} %collective-permute-done.6, ...), kind=kLoop, calls=%fused_computation.105 | loop fusion | flops 37748736 | bytes 23433216 | tf_op jit(solution)/shard_map/add | solution.py:42
  100.7 4.2 %collective-permute-done.12 = f32[1,8,8,128]{3,2,1,0:T(8,128)S(1)} collective-permute-done((f32[1,8,8,128]{3,2,1,0:T(8,128)S(1)}, f32[1,8,8,128]{3,2,1,0:T(8,128)S(1)}, u32[]{:S(2)}, u32[]{:S(2)}) %collective-permute-start.12) | collective-permute-done | bytes 32800 | tf_op jit(solution)/shard_map/ppermute | solution.py:17
  105.1 7.2 %collective-permute-start.15 = (f32[130,1,8,128]{3,2,1,0:T(8,128)S(1)}, f32[130,1,8,128]{3,2,1,0:T(8,128)S(1)}, u32[]{:S(2)}, u32[]{:S(2)}) collective-permute-start(f32[130,1,8,128]{3,2,1,0:T(8,128)S(1)} %get-tuple-element.24), channel_id=1, source_target_pairs={{0,4},{4,8},{8,12},{1,5},{5,9},{9,13},{2,6},{6,10},{10,14},{3,7},{... | collective-permute-start | bytes 1597448 | tf_op jit(solution)/shard_map/ppermute | solution.py:14
  119.7 5.2 %collective-permute-start.17 = (f32[130,10,1,128]{3,0,2,1:T(8,128)S(1)}, f32[130,10,1,128]{3,0,2,1:T(8,128)S(1)}, u32[]{:S(2)}, u32[]{:S(2)}) collective-permute-start(f32[130,10,1,128]{3,0,2,1:T(8,128)S(1)} %copy.43), channel_id=1, source_target_pairs={{0,1},{1,2},{2,3},{4,5},{5,6},{6,7},{8,9},{9,10},{10,11},{12,13},{... | collective-permute-start | bytes 1996808 | tf_op jit(solution)/shard_map/ppermute | solution.py:14
  124.9 7.3 %collective-permute-done.16 = f32[130,10,1,128]{3,0,2,1:T(8,128)S(1)} collective-permute-done((f32[130,10,1,128]{3,0,2,1:T(8,128)S(1)}, f32[130,10,1,128]{3,0,2,1:T(8,128)S(1)}, u32[]{:S(2)}, u32[]{:S(2)}) %collective-permute-start.16) | collective-permute-done | bytes 665632 | tf_op jit(solution)/shard_map/ppermute | solution.py:17
  134.8 10.8 %multiply_add_fusion.3 = f32[128,8,8,128]{3,2,1,0:T(8,128)S(1)} fusion(f32[128,8,8,128]{3,2,1,0:T(8,128)S(1)} %multiply_add_fusion.4, f32[128,8,8,128]{3,2,1,0:T(8,128)S(1)} %copy-done, f32[130,10,1,128]{3,2,1,0:T(1,128)S(1)} %copy.42, f32[130,1,8,128]{3,2,1,0:T(8,128)} %copy-done.14, f32[1,8,8,128]{3,2,1,0:T(8,128)S(1)} %collective-permute-done.12, ...), kind=kLoop, calls=%fused_computation.104 | loop fusion | flops 37748736 | bytes 23433216 | tf_op jit(solution)/shard_map/add | solution.py:42
  148.8 4.2 %collective-permute-done.18 = f32[1,8,8,128]{3,2,1,0:T(8,128)S(1)} collective-permute-done((f32[1,8,8,128]{3,2,1,0:T(8,128)S(1)}, f32[1,8,8,128]{3,2,1,0:T(8,128)S(1)}, u32[]{:S(2)}, u32[]{:S(2)}) %collective-permute-start.18) | collective-permute-done | bytes 32800 | tf_op jit(solution)/shard_map/ppermute | solution.py:17
  153.1 7.2 %collective-permute-start.21 = (f32[130,1,8,128]{3,2,1,0:T(8,128)S(1)}, f32[130,1,8,128]{3,2,1,0:T(8,128)S(1)}, u32[]{:S(2)}, u32[]{:S(2)}) collective-permute-start(f32[130,1,8,128]{3,2,1,0:T(8,128)S(1)} %get-tuple-element.22), channel_id=1, source_target_pairs={{0,4},{4,8},{8,12},{1,5},{5,9},{9,13},{2,6},{6,10},{10,14},{3,7},{... | collective-permute-start | bytes 1597448 | tf_op jit(solution)/shard_map/ppermute | solution.py:14
  167.7 5.1 %collective-permute-start.23 = (f32[130,10,1,128]{3,0,2,1:T(8,128)S(1)}, f32[130,10,1,128]{3,0,2,1:T(8,128)S(1)}, u32[]{:S(2)}, u32[]{:S(2)}) collective-permute-start(f32[130,10,1,128]{3,0,2,1:T(8,128)S(1)} %copy.47), channel_id=1, source_target_pairs={{0,1},{1,2},{2,3},{4,5},{5,6},{6,7},{8,9},{9,10},{10,11},{12,13},{... | collective-permute-start | bytes 1996808 | tf_op jit(solution)/shard_map/ppermute | solution.py:14
  172.7 7.5 %collective-permute-done.22 = f32[130,10,1,128]{3,0,2,1:T(8,128)S(1)} collective-permute-done((f32[130,10,1,128]{3,0,2,1:T(8,128)S(1)}, f32[130,10,1,128]{3,0,2,1:T(8,128)S(1)}, u32[]{:S(2)}, u32[]{:S(2)}) %collective-permute-start.22) | collective-permute-done | bytes 665632 | tf_op jit(solution)/shard_map/ppermute | solution.py:17
  182.8 10.8 %multiply_add_fusion.2 = f32[128,8,8,128]{3,2,1,0:T(8,128)S(1)} fusion(f32[128,8,8,128]{3,2,1,0:T(8,128)S(1)} %multiply_add_fusion.3, f32[128,8,8,128]{3,2,1,0:T(8,128)S(1)} %copy-done, f32[130,10,1,128]{3,2,1,0:T(1,128)S(1)} %copy.46, f32[130,1,8,128]{3,2,1,0:T(8,128)} %copy-done.15, f32[1,8,8,128]{3,2,1,0:T(8,128)S(1)} %collective-permute-done.18, ...), kind=kLoop, calls=%fused_computation.103 | loop fusion | flops 37748736 | bytes 23433216 | tf_op jit(solution)/shard_map/add | solution.py:42
  196.8 4.2 %collective-permute-done.24 = f32[1,8,8,128]{3,2,1,0:T(8,128)S(1)} collective-permute-done((f32[1,8,8,128]{3,2,1,0:T(8,128)S(1)}, f32[1,8,8,128]{3,2,1,0:T(8,128)S(1)}, u32[]{:S(2)}, u32[]{:S(2)}) %collective-permute-start.24) | collective-permute-done | bytes 32800 | tf_op jit(solution)/shard_map/ppermute | solution.py:17
  201.1 7.2 %collective-permute-start.27 = (f32[130,1,8,128]{3,2,1,0:T(8,128)S(1)}, f32[130,1,8,128]{3,2,1,0:T(8,128)S(1)}, u32[]{:S(2)}, u32[]{:S(2)}) collective-permute-start(f32[130,1,8,128]{3,2,1,0:T(8,128)S(1)} %get-tuple-element.20), channel_id=1, source_target_pairs={{0,4},{4,8},{8,12},{1,5},{5,9},{9,13},{2,6},{6,10},{10,14},{3,7},{... | collective-permute-start | bytes 1597448 | tf_op jit(solution)/shard_map/ppermute | solution.py:14
  216.0 5.1 %collective-permute-start.29 = (f32[130,10,1,128]{3,0,2,1:T(8,128)S(1)}, f32[130,10,1,128]{3,0,2,1:T(8,128)S(1)}, u32[]{:S(2)}, u32[]{:S(2)}) collective-permute-start(f32[130,10,1,128]{3,0,2,1:T(8,128)S(1)} %copy.51), channel_id=1, source_target_pairs={{0,1},{1,2},{2,3},{4,5},{5,6},{6,7},{8,9},{9,10},{10,11},{12,13},{... | collective-permute-start | bytes 1996808 | tf_op jit(solution)/shard_map/ppermute | solution.py:14
  221.0 7.5 %collective-permute-done.28 = f32[130,10,1,128]{3,0,2,1:T(8,128)S(1)} collective-permute-done((f32[130,10,1,128]{3,0,2,1:T(8,128)S(1)}, f32[130,10,1,128]{3,0,2,1:T(8,128)S(1)}, u32[]{:S(2)}, u32[]{:S(2)}) %collective-permute-start.28) | collective-permute-done | bytes 665632 | tf_op jit(solution)/shard_map/ppermute | solution.py:17
  231.1 10.8 %multiply_add_fusion.1 = f32[128,8,8,128]{3,2,1,0:T(8,128)S(1)} fusion(f32[128,8,8,128]{3,2,1,0:T(8,128)S(1)} %copy-done.4, f32[128,8,8,128]{3,2,1,0:T(8,128)S(1)} %copy-done, f32[130,10,1,128]{3,2,1,0:T(1,128)S(1)} %copy.50, f32[130,1,8,128]{3,2,1,0:T(8,128)} %copy-done.16, f32[1,8,8,128]{3,2,1,0:T(8,128)S(1)} %collective-permute-done.24, ...), kind=kLoop, calls=%fused_computation.102 | loop fusion | flops 37748736 | bytes 23433216 | tf_op jit(solution)/shard_map/add | solution.py:42
  245.1 4.2 %collective-permute-done.30 = f32[1,8,8,128]{3,2,1,0:T(8,128)S(1)} collective-permute-done((f32[1,8,8,128]{3,2,1,0:T(8,128)S(1)}, f32[1,8,8,128]{3,2,1,0:T(8,128)S(1)}, u32[]{:S(2)}, u32[]{:S(2)}) %collective-permute-start.30) | collective-permute-done | bytes 32800 | tf_op jit(solution)/shard_map/ppermute | solution.py:17
  249.4 7.2 %collective-permute-start.33 = (f32[130,1,8,128]{3,2,1,0:T(8,128)S(1)}, f32[130,1,8,128]{3,2,1,0:T(8,128)S(1)}, u32[]{:S(2)}, u32[]{:S(2)}) collective-permute-start(f32[130,1,8,128]{3,2,1,0:T(8,128)S(1)} %get-tuple-element.18), channel_id=1, source_target_pairs={{0,4},{4,8},{8,12},{1,5},{5,9},{9,13},{2,6},{6,10},{10,14},{3,7},{... | collective-permute-start | bytes 1597448 | tf_op jit(solution)/shard_map/ppermute | solution.py:14
  262.6 4.4 %collective-permute-start.35 = (f32[130,10,1,128]{3,0,2,1:T(8,128)S(1)}, f32[130,10,1,128]{3,0,2,1:T(8,128)S(1)}, u32[]{:S(2)}, u32[]{:S(2)}) collective-permute-start(f32[130,10,1,128]{3,0,2,1:T(8,128)S(1)} %copy.55), channel_id=1, source_target_pairs={{0,1},{1,2},{2,3},{4,5},{5,6},{6,7},{8,9},{9,10},{10,11},{12,13},{... | collective-permute-start | bytes 1996808 | tf_op jit(solution)/shard_map/ppermute | solution.py:14
  268.4 8.0 %collective-permute-done.35 = f32[130,10,1,128]{3,0,2,1:T(8,128)S(1)} collective-permute-done((f32[130,10,1,128]{3,0,2,1:T(8,128)S(1)}, f32[130,10,1,128]{3,0,2,1:T(8,128)S(1)}, u32[]{:S(2)}, u32[]{:S(2)}) %collective-permute-start.35) | collective-permute-done | bytes 665632 | tf_op jit(solution)/shard_map/ppermute | solution.py:14
  281.6 11.0 %fusion = (f32[8,8,128]{2,1,0:T(8,128)S(1)}, f32[128,8,8,128]{3,2,1,0:T(8,128)}) fusion(f32[128,8,8,128]{3,2,1,0:T(8,128)S(1)} %multiply_add_fusion.1, f32[128,8,8,128]{3,2,1,0:T(8,128)S(1)} %copy-done, f32[130,1,8,128]{3,2,1,0:T(8,128)S(1)} %collective-permute-done.32, f32[1,8,8,128]{3,2,1,0:T(8,128)S(1)} %collective-permute-done.30, ...), kind=kLoop, calls=%fused_computation.156 | loop fusion | flops 38789120 | bytes 23465984 | tf_op jit(solution)/shard_map/reduce_sum | solution.py:51
  292.6 6.9 %psum.14 = f32[1,8,8,128]{3,2,1,0:T(8,128)S(1)} all-reduce(f32[1,8,8,128]{3,2,1,0:T(8,128)S(1)} %bitcast.6), channel_id=1, replica_groups=mesh['south'=2,'east'=4,'down'=4] {'south'}, use_global_device_ids=true, to_apply=%region_1.0 | all-reduce | flops 8192 | bytes 65536 | tf_op jit(solution)/shard_map/psum | solution.py:51
  302.2 8.9 %psum.15 = f32[1,8,8,128]{3,2,1,0:T(8,128)S(1)} all-reduce(f32[1,8,8,128]{3,2,1,0:T(8,128)S(1)} %bitcast.7), channel_id=1, replica_groups=mesh['south'=2,'east'=4,'down'=4] {'south'}, use_global_device_ids=true, to_apply=%region_3.0 | all-reduce | flops 8192 | bytes 65536 | tf_op jit(solution)/shard_map/psum | solution.py:53
  311.2 5.1 %subtract_multiply_fusion = f32[128,8,8,128]{3,2,1,0:T(8,128)} fusion(f32[128,8,8,128]{3,2,1,0:T(8,128)} %get-tuple-element.5, f32[8,8,128]{2,1,0:T(8,128)S(1)} %rsqrt_bitcast_fusion, f32[8,8,128]{2,1,0:T(8,128)S(1)} %multiply_bitcast_fusion), kind=kLoop, calls=%fused_computation.107 | loop fusion | flops 2097152 | bytes 8454144 | tf_op jit(solution)/shard_map/mul | solution.py:54
  (131 shorter events, 91.1 us)
Async XLA Ops:
  1.4 6.4 %collective-permute-start.1 = (f32[1,8,8,128]{3,2,1,0:T(8,128)S(1)}, f32[1,8,8,128]{3,2,1,0:T(8,128)S(1)}, u32[]{:S(2)}, u32[]{:S(2)}) collective-permute-start(f32[1,8,8,128]{3,2,1,0:T(8,128)S(1)} %get-tuple-element.41), channel_id=1, source_target_pairs={{0,16},{1,17},{2,18},{3,19},{4,20},{5,21},{6,22},{7,23},{8,24},{9,... | collective-permute-start | bytes 98312 | tf_op jit(solution)/shard_map/ppermute | solution.py:14
  6.3 5.8 %collective-permute-start = (f32[1,8,8,128]{3,2,1,0:T(8,128)S(1)}, f32[1,8,8,128]{3,2,1,0:T(8,128)S(1)}, u32[]{:S(2)}, u32[]{:S(2)}) collective-permute-start(f32[1,8,8,128]{3,2,1,0:T(8,128)S(1)} %get-tuple-element.40), channel_id=1, source_target_pairs={{16,0},{17,1},{18,2},{19,3},{20,4},{21,5},{22,6},{23,7},{24,8},{25... | collective-permute-start | bytes 98312 | tf_op jit(solution)/shard_map/ppermute | solution.py:17
  13.8 5.5 %collective-permute-start.2 = (f32[130,1,8,128]{3,2,1,0:T(8,128)S(1)}, f32[130,1,8,128]{3,2,1,0:T(8,128)S(1)}, u32[]{:S(2)}, u32[]{:S(2)}) collective-permute-start(f32[130,1,8,128]{3,2,1,0:T(8,128)S(1)} %get-tuple-element.29), channel_id=1, source_target_pairs={{4,0},{8,4},{12,8},{5,1},{9,5},{13,9},{6,2},{10,6},{14,10},{7,3},{... | collective-permute-start | bytes 1597448 | tf_op jit(solution)/shard_map/ppermute | solution.py:17
  20.5 14.0 %collective-permute-start.4 = (f32[130,10,1,128]{3,0,2,1:T(8,128)S(1)}, f32[130,10,1,128]{3,0,2,1:T(8,128)S(1)}, u32[]{:S(2)}, u32[]{:S(2)}) collective-permute-start(f32[130,10,1,128]{3,0,2,1:T(8,128)S(1)} %copy.33), channel_id=1, source_target_pairs={{1,0},{2,1},{3,2},{5,4},{6,5},{7,6},{9,8},{10,9},{11,10},{13,12},{... | collective-permute-start | bytes 1996808 | tf_op jit(solution)/shard_map/ppermute | solution.py:17
  22.1 14.2 %collective-permute-start.5 = (f32[130,10,1,128]{3,0,2,1:T(8,128)S(1)}, f32[130,10,1,128]{3,0,2,1:T(8,128)S(1)}, u32[]{:S(2)}, u32[]{:S(2)}) collective-permute-start(f32[130,10,1,128]{3,0,2,1:T(8,128)S(1)} %copy.35), channel_id=1, source_target_pairs={{0,1},{1,2},{2,3},{4,5},{5,6},{6,7},{8,9},{9,10},{10,11},{12,13},{... | collective-permute-start | bytes 1996808 | tf_op jit(solution)/shard_map/ppermute | solution.py:14
  48.7 4.4 %collective-permute-start.7 = (f32[1,8,8,128]{3,2,1,0:T(8,128)S(1)}, f32[1,8,8,128]{3,2,1,0:T(8,128)S(1)}, u32[]{:S(2)}, u32[]{:S(2)}) collective-permute-start(f32[1,8,8,128]{3,2,1,0:T(8,128)S(1)} %get-tuple-element.38), channel_id=1, source_target_pairs={{0,16},{1,17},{2,18},{3,19},{4,20},{5,21},{6,22},{7,23},{8,24},{9,... | collective-permute-start | bytes 98312 | tf_op jit(solution)/shard_map/ppermute | solution.py:14
  51.5 5.8 %collective-permute-start.6 = (f32[1,8,8,128]{3,2,1,0:T(8,128)S(1)}, f32[1,8,8,128]{3,2,1,0:T(8,128)S(1)}, u32[]{:S(2)}, u32[]{:S(2)}) collective-permute-start(f32[1,8,8,128]{3,2,1,0:T(8,128)S(1)} %get-tuple-element.39), channel_id=1, source_target_pairs={{16,0},{17,1},{18,2},{19,3},{20,4},{21,5},{22,6},{23,7},{24,8},{25... | collective-permute-start | bytes 98312 | tf_op jit(solution)/shard_map/ppermute | solution.py:17
  57.4 8.4 %collective-permute-start.9 = (f32[130,1,8,128]{3,2,1,0:T(8,128)S(1)}, f32[130,1,8,128]{3,2,1,0:T(8,128)S(1)}, u32[]{:S(2)}, u32[]{:S(2)}) collective-permute-start(f32[130,1,8,128]{3,2,1,0:T(8,128)S(1)} %get-tuple-element.26), channel_id=1, source_target_pairs={{0,4},{4,8},{8,12},{1,5},{5,9},{9,13},{2,6},{6,10},{10,14},{3,7},{... | collective-permute-start | bytes 1597448 | tf_op jit(solution)/shard_map/ppermute | solution.py:14
  64.3 4.3 %collective-permute-start.8 = (f32[130,1,8,128]{3,2,1,0:T(8,128)S(1)}, f32[130,1,8,128]{3,2,1,0:T(8,128)S(1)}, u32[]{:S(2)}, u32[]{:S(2)}) collective-permute-start(f32[130,1,8,128]{3,2,1,0:T(8,128)S(1)} %get-tuple-element.27), channel_id=1, source_target_pairs={{4,0},{8,4},{12,8},{5,1},{9,5},{13,9},{6,2},{10,6},{14,10},{7,3},{... | collective-permute-start | bytes 1597448 | tf_op jit(solution)/shard_map/ppermute | solution.py:17
  70.3 14.0 %collective-permute-start.10 = (f32[130,10,1,128]{3,0,2,1:T(8,128)S(1)}, f32[130,10,1,128]{3,0,2,1:T(8,128)S(1)}, u32[]{:S(2)}, u32[]{:S(2)}) collective-permute-start(f32[130,10,1,128]{3,0,2,1:T(8,128)S(1)} %copy.37), channel_id=1, source_target_pairs={{1,0},{2,1},{3,2},{5,4},{6,5},{7,6},{9,8},{10,9},{11,10},{13,12},{... | collective-permute-start | bytes 1996808 | tf_op jit(solution)/shard_map/ppermute | solution.py:17
  71.6 14.4 %collective-permute-start.11 = (f32[130,10,1,128]{3,0,2,1:T(8,128)S(1)}, f32[130,10,1,128]{3,0,2,1:T(8,128)S(1)}, u32[]{:S(2)}, u32[]{:S(2)}) collective-permute-start(f32[130,10,1,128]{3,0,2,1:T(8,128)S(1)} %copy.39), channel_id=1, source_target_pairs={{0,1},{1,2},{2,3},{4,5},{5,6},{6,7},{8,9},{9,10},{10,11},{12,13},{... | collective-permute-start | bytes 1996808 | tf_op jit(solution)/shard_map/ppermute | solution.py:14
  97.5 3.2 %collective-permute-start.13 = (f32[1,8,8,128]{3,2,1,0:T(8,128)S(1)}, f32[1,8,8,128]{3,2,1,0:T(8,128)S(1)}, u32[]{:S(2)}, u32[]{:S(2)}) collective-permute-start(f32[1,8,8,128]{3,2,1,0:T(8,128)S(1)} %get-tuple-element.36), channel_id=1, source_target_pairs={{0,16},{1,17},{2,18},{3,19},{4,20},{5,21},{6,22},{7,23},{8,24},{9,... | collective-permute-start | bytes 98312 | tf_op jit(solution)/shard_map/ppermute | solution.py:14
  99.2 5.8 %collective-permute-start.12 = (f32[1,8,8,128]{3,2,1,0:T(8,128)S(1)}, f32[1,8,8,128]{3,2,1,0:T(8,128)S(1)}, u32[]{:S(2)}, u32[]{:S(2)}) collective-permute-start(f32[1,8,8,128]{3,2,1,0:T(8,128)S(1)} %get-tuple-element.37), channel_id=1, source_target_pairs={{16,0},{17,1},{18,2},{19,3},{20,4},{21,5},{22,6},{23,7},{24,8},{25... | collective-permute-start | bytes 98312 | tf_op jit(solution)/shard_map/ppermute | solution.py:17
  105.1 8.7 %collective-permute-start.15 = (f32[130,1,8,128]{3,2,1,0:T(8,128)S(1)}, f32[130,1,8,128]{3,2,1,0:T(8,128)S(1)}, u32[]{:S(2)}, u32[]{:S(2)}) collective-permute-start(f32[130,1,8,128]{3,2,1,0:T(8,128)S(1)} %get-tuple-element.24), channel_id=1, source_target_pairs={{0,4},{4,8},{8,12},{1,5},{5,9},{9,13},{2,6},{6,10},{10,14},{3,7},{... | collective-permute-start | bytes 1597448 | tf_op jit(solution)/shard_map/ppermute | solution.py:14
  112.3 4.3 %collective-permute-start.14 = (f32[130,1,8,128]{3,2,1,0:T(8,128)S(1)}, f32[130,1,8,128]{3,2,1,0:T(8,128)S(1)}, u32[]{:S(2)}, u32[]{:S(2)}) collective-permute-start(f32[130,1,8,128]{3,2,1,0:T(8,128)S(1)} %get-tuple-element.25), channel_id=1, source_target_pairs={{4,0},{8,4},{12,8},{5,1},{9,5},{13,9},{6,2},{10,6},{14,10},{7,3},{... | collective-permute-start | bytes 1597448 | tf_op jit(solution)/shard_map/ppermute | solution.py:17
  118.3 14.0 %collective-permute-start.16 = (f32[130,10,1,128]{3,0,2,1:T(8,128)S(1)}, f32[130,10,1,128]{3,0,2,1:T(8,128)S(1)}, u32[]{:S(2)}, u32[]{:S(2)}) collective-permute-start(f32[130,10,1,128]{3,0,2,1:T(8,128)S(1)} %copy.41), channel_id=1, source_target_pairs={{1,0},{2,1},{3,2},{5,4},{6,5},{7,6},{9,8},{10,9},{11,10},{13,12},{... | collective-permute-start | bytes 1996808 | tf_op jit(solution)/shard_map/ppermute | solution.py:17
  119.7 14.4 %collective-permute-start.17 = (f32[130,10,1,128]{3,0,2,1:T(8,128)S(1)}, f32[130,10,1,128]{3,0,2,1:T(8,128)S(1)}, u32[]{:S(2)}, u32[]{:S(2)}) collective-permute-start(f32[130,10,1,128]{3,0,2,1:T(8,128)S(1)} %copy.43), channel_id=1, source_target_pairs={{0,1},{1,2},{2,3},{4,5},{5,6},{6,7},{8,9},{9,10},{10,11},{12,13},{... | collective-permute-start | bytes 1996808 | tf_op jit(solution)/shard_map/ppermute | solution.py:14
  147.2 5.8 %collective-permute-start.18 = (f32[1,8,8,128]{3,2,1,0:T(8,128)S(1)}, f32[1,8,8,128]{3,2,1,0:T(8,128)S(1)}, u32[]{:S(2)}, u32[]{:S(2)}) collective-permute-start(f32[1,8,8,128]{3,2,1,0:T(8,128)S(1)} %get-tuple-element.35), channel_id=1, source_target_pairs={{16,0},{17,1},{18,2},{19,3},{20,4},{21,5},{22,6},{23,7},{24,8},{25... | collective-permute-start | bytes 98312 | tf_op jit(solution)/shard_map/ppermute | solution.py:17
  153.1 8.7 %collective-permute-start.21 = (f32[130,1,8,128]{3,2,1,0:T(8,128)S(1)}, f32[130,1,8,128]{3,2,1,0:T(8,128)S(1)}, u32[]{:S(2)}, u32[]{:S(2)}) collective-permute-start(f32[130,1,8,128]{3,2,1,0:T(8,128)S(1)} %get-tuple-element.22), channel_id=1, source_target_pairs={{0,4},{4,8},{8,12},{1,5},{5,9},{9,13},{2,6},{6,10},{10,14},{3,7},{... | collective-permute-start | bytes 1597448 | tf_op jit(solution)/shard_map/ppermute | solution.py:14
  160.3 4.3 %collective-permute-start.20 = (f32[130,1,8,128]{3,2,1,0:T(8,128)S(1)}, f32[130,1,8,128]{3,2,1,0:T(8,128)S(1)}, u32[]{:S(2)}, u32[]{:S(2)}) collective-permute-start(f32[130,1,8,128]{3,2,1,0:T(8,128)S(1)} %get-tuple-element.23), channel_id=1, source_target_pairs={{4,0},{8,4},{12,8},{5,1},{9,5},{13,9},{6,2},{10,6},{14,10},{7,3},{... | collective-permute-start | bytes 1597448 | tf_op jit(solution)/shard_map/ppermute | solution.py:17
  166.3 14.0 %collective-permute-start.22 = (f32[130,10,1,128]{3,0,2,1:T(8,128)S(1)}, f32[130,10,1,128]{3,0,2,1:T(8,128)S(1)}, u32[]{:S(2)}, u32[]{:S(2)}) collective-permute-start(f32[130,10,1,128]{3,0,2,1:T(8,128)S(1)} %copy.45), channel_id=1, source_target_pairs={{1,0},{2,1},{3,2},{5,4},{6,5},{7,6},{9,8},{10,9},{11,10},{13,12},{... | collective-permute-start | bytes 1996808 | tf_op jit(solution)/shard_map/ppermute | solution.py:17
  167.7 14.4 %collective-permute-start.23 = (f32[130,10,1,128]{3,0,2,1:T(8,128)S(1)}, f32[130,10,1,128]{3,0,2,1:T(8,128)S(1)}, u32[]{:S(2)}, u32[]{:S(2)}) collective-permute-start(f32[130,10,1,128]{3,0,2,1:T(8,128)S(1)} %copy.47), channel_id=1, source_target_pairs={{0,1},{1,2},{2,3},{4,5},{5,6},{6,7},{8,9},{9,10},{10,11},{12,13},{... | collective-permute-start | bytes 1996808 | tf_op jit(solution)/shard_map/ppermute | solution.py:14
  195.2 5.8 %collective-permute-start.24 = (f32[1,8,8,128]{3,2,1,0:T(8,128)S(1)}, f32[1,8,8,128]{3,2,1,0:T(8,128)S(1)}, u32[]{:S(2)}, u32[]{:S(2)}) collective-permute-start(f32[1,8,8,128]{3,2,1,0:T(8,128)S(1)} %get-tuple-element.33), channel_id=1, source_target_pairs={{16,0},{17,1},{18,2},{19,3},{20,4},{21,5},{22,6},{23,7},{24,8},{25... | collective-permute-start | bytes 98312 | tf_op jit(solution)/shard_map/ppermute | solution.py:17
  201.1 8.7 %collective-permute-start.27 = (f32[130,1,8,128]{3,2,1,0:T(8,128)S(1)}, f32[130,1,8,128]{3,2,1,0:T(8,128)S(1)}, u32[]{:S(2)}, u32[]{:S(2)}) collective-permute-start(f32[130,1,8,128]{3,2,1,0:T(8,128)S(1)} %get-tuple-element.20), channel_id=1, source_target_pairs={{0,4},{4,8},{8,12},{1,5},{5,9},{9,13},{2,6},{6,10},{10,14},{3,7},{... | collective-permute-start | bytes 1597448 | tf_op jit(solution)/shard_map/ppermute | solution.py:14
  208.3 4.3 %collective-permute-start.26 = (f32[130,1,8,128]{3,2,1,0:T(8,128)S(1)}, f32[130,1,8,128]{3,2,1,0:T(8,128)S(1)}, u32[]{:S(2)}, u32[]{:S(2)}) collective-permute-start(f32[130,1,8,128]{3,2,1,0:T(8,128)S(1)} %get-tuple-element.21), channel_id=1, source_target_pairs={{4,0},{8,4},{12,8},{5,1},{9,5},{13,9},{6,2},{10,6},{14,10},{7,3},{... | collective-permute-start | bytes 1597448 | tf_op jit(solution)/shard_map/ppermute | solution.py:17
  214.3 14.2 %collective-permute-start.28 = (f32[130,10,1,128]{3,0,2,1:T(8,128)S(1)}, f32[130,10,1,128]{3,0,2,1:T(8,128)S(1)}, u32[]{:S(2)}, u32[]{:S(2)}) collective-permute-start(f32[130,10,1,128]{3,0,2,1:T(8,128)S(1)} %copy.49), channel_id=1, source_target_pairs={{1,0},{2,1},{3,2},{5,4},{6,5},{7,6},{9,8},{10,9},{11,10},{13,12},{... | collective-permute-start | bytes 1996808 | tf_op jit(solution)/shard_map/ppermute | solution.py:17
  216.0 14.4 %collective-permute-start.29 = (f32[130,10,1,128]{3,0,2,1:T(8,128)S(1)}, f32[130,10,1,128]{3,0,2,1:T(8,128)S(1)}, u32[]{:S(2)}, u32[]{:S(2)}) collective-permute-start(f32[130,10,1,128]{3,0,2,1:T(8,128)S(1)} %copy.51), channel_id=1, source_target_pairs={{0,1},{1,2},{2,3},{4,5},{5,6},{6,7},{8,9},{9,10},{10,11},{12,13},{... | collective-permute-start | bytes 1996808 | tf_op jit(solution)/shard_map/ppermute | solution.py:14
  243.5 5.8 %collective-permute-start.30 = (f32[1,8,8,128]{3,2,1,0:T(8,128)S(1)}, f32[1,8,8,128]{3,2,1,0:T(8,128)S(1)}, u32[]{:S(2)}, u32[]{:S(2)}) collective-permute-start(f32[1,8,8,128]{3,2,1,0:T(8,128)S(1)} %get-tuple-element.31), channel_id=1, source_target_pairs={{16,0},{17,1},{18,2},{19,3},{20,4},{21,5},{22,6},{23,7},{24,8},{25... | collective-permute-start | bytes 98312 | tf_op jit(solution)/shard_map/ppermute | solution.py:17
  249.4 8.8 %collective-permute-start.33 = (f32[130,1,8,128]{3,2,1,0:T(8,128)S(1)}, f32[130,1,8,128]{3,2,1,0:T(8,128)S(1)}, u32[]{:S(2)}, u32[]{:S(2)}) collective-permute-start(f32[130,1,8,128]{3,2,1,0:T(8,128)S(1)} %get-tuple-element.18), channel_id=1, source_target_pairs={{0,4},{4,8},{8,12},{1,5},{5,9},{9,13},{2,6},{6,10},{10,14},{3,7},{... | collective-permute-start | bytes 1597448 | tf_op jit(solution)/shard_map/ppermute | solution.py:14
  256.6 4.3 %collective-permute-start.32 = (f32[130,1,8,128]{3,2,1,0:T(8,128)S(1)}, f32[130,1,8,128]{3,2,1,0:T(8,128)S(1)}, u32[]{:S(2)}, u32[]{:S(2)}) collective-permute-start(f32[130,1,8,128]{3,2,1,0:T(8,128)S(1)} %get-tuple-element.19), channel_id=1, source_target_pairs={{4,0},{8,4},{12,8},{5,1},{9,5},{13,9},{6,2},{10,6},{14,10},{7,3},{... | collective-permute-start | bytes 1597448 | tf_op jit(solution)/shard_map/ppermute | solution.py:17
  262.6 13.8 %collective-permute-start.35 = (f32[130,10,1,128]{3,0,2,1:T(8,128)S(1)}, f32[130,10,1,128]{3,0,2,1:T(8,128)S(1)}, u32[]{:S(2)}, u32[]{:S(2)}) collective-permute-start(f32[130,10,1,128]{3,0,2,1:T(8,128)S(1)} %copy.55), channel_id=1, source_target_pairs={{0,1},{1,2},{2,3},{4,5},{5,6},{6,7},{8,9},{9,10},{10,11},{12,13},{... | collective-permute-start | bytes 1996808 | tf_op jit(solution)/shard_map/ppermute | solution.py:14
  267.1 13.9 %collective-permute-start.34 = (f32[130,10,1,128]{3,0,2,1:T(8,128)S(1)}, f32[130,10,1,128]{3,0,2,1:T(8,128)S(1)}, u32[]{:S(2)}, u32[]{:S(2)}) collective-permute-start(f32[130,10,1,128]{3,0,2,1:T(8,128)S(1)} %copy.53), channel_id=1, source_target_pairs={{1,0},{2,1},{3,2},{5,4},{6,5},{7,6},{9,8},{10,9},{11,10},{13,12},{... | collective-permute-start | bytes 1996808 | tf_op jit(solution)/shard_map/ppermute | solution.py:17
  (21 other events, 237.3 us)
where the time goes:
time: 321 us; the launch traced here: 316 us
  starting transfers between devices  105 us (33%)
  waiting for transfers between devices  98.2 us (31%)
  other arithmetic  83.1 us (26%)
  blocking collectives  15.8 us (5%)
  local copies, waits for them, and re-layouts  12.4 us (4%)
    ppermute x18, waiting for transfers between devices, extended(): lax.ppermute(lax.slice_in_dim(block, 0, width, axis=dim), axis, backward)  82.1 us
    ppermute x18, starting transfers between devices, extended(): lax.ppermute(lax.slice_in_dim(block, block.shape[dim] - width, None, axis...  80.9 us
    add x5, other arithmetic, advance(): middle - flow_j * slopes[0] - flow_i * slopes[1] - flow_k * slopes[2]  54.7 us
    ppermute x18, starting transfers between devices, extended(): lax.ppermute(lax.slice_in_dim(block, 0, width, axis=dim), axis, backward)  24.3 us
    ppermute x18, waiting for transfers between devices, extended(): lax.ppermute(lax.slice_in_dim(block, block.shape[dim] - width, None, axis...  16.1 us
    reduce_sum x1, other arithmetic, per_device(): jnp.sum(field_values, axis=0, keepdims=True)  11 us
    psum x1, blocking collectives, per_device(): lax.psum(jnp.sum(centred * centred, axis=0, keepdims=True), 'south') / count  8.94 us
    concatenate x10, other arithmetic, extended(): block = jnp.concatenate([low, block, high], axis=dim)  8.01 us
  transfers between devices with their start and end apart: 36, of which 34 were waited for; matrix products, arithmetic and copies ran while one was open for 2% of the time, Pallas kernels for 0%

commit v1 on v0

v1 whole, which is shorter than its diff:
```python
import functools

import jax
import jax.numpy as jnp
from jax import lax
from jax.experimental import pallas as pl
from jax.experimental.pallas import tpu as pltpu
from jax.sharding import PartitionSpec as P

STEPS = 6
PIECES = 8
MESH = pl.DeviceIdType.MESH


def transport(counts, pieces, steps, field, flow_j, flow_i, flow_k, end, mean_out, scale_out,
              cells, flows, face_out, face_in, stats,
              load_sem, flow_sem, end_sem, k_send, k_recv, i_send, i_recv, j_send, j_recv,
              stat_send, stat_recv):
    n_south, n_east, n_down = counts
    nj, ni, nk, _ = field.shape
    rows = nj // pieces
    south, east, down = (lax.axis_index(a) for a in ("south", "east", "down"))
    place = {"south": (south, n_south), "east": (east, n_east), "down": (down, n_down)}
    downward = lax.rem(south, 2) == 0

    def has(axis, side):
        me, count = place[axis]
        return me > 0 if side == 0 else me < count - 1

    def beside(axis, side):
        me, _ = place[axis]
        return {axis: me - 1 if side == 0 else me + 1}

    def piece_of(c):
        return jnp.where(downward, pieces - 1 - c, c)

    def load(c):
        return pltpu.make_async_copy(
            field.at[pl.ds(c * rows, rows)],
            cells.at[0, pl.ds(c * rows + 1, rows), pl.ds(1, ni)],
            load_sem.at[c],
        )

    def load_flow(d, c):
        source = (flow_j, flow_i, flow_k)[d]
        part = pl.ds(c * rows, rows)
        return pltpu.make_async_copy(source.at[part], flows.at[d, part], flow_sem.at[d, c])

    def k_copy(slot, side, c):
        part = pl.ds(c * rows, rows)
        return pltpu.make_async_remote_copy(
            face_out.at[slot, side, part], face_in.at[slot, 1 - side, part],
            k_send.at[slot, side, c], k_recv.at[slot, 1 - side, c],
            device_id=beside("down", side), device_id_type=MESH,
        )

    def i_copy(slot, side, c):
        part = pl.ds(c * rows + 1, rows)
        return pltpu.make_async_remote_copy(
            cells.at[slot, part, 1 if side == 0 else ni],
            cells.at[slot, part, ni + 1 if side == 0 else 0],
            i_send.at[slot, side, c], i_recv.at[slot, 1 - side, c],
            device_id=beside("east", side), device_id_type=MESH,
        )

    def j_copy(slot, side):
        return pltpu.make_async_remote_copy(
            cells.at[slot, 1 if side == 0 else nj, pl.ds(1, ni)],
            cells.at[slot, nj + 1 if side == 0 else 0, pl.ds(1, ni)],
            j_send.at[slot, side], j_recv.at[slot, 1 - side],
            device_id=beside("south", side), device_id_type=MESH,
        )

    def each_copy(slot, c, act):
        for side in (0, 1):
            pl.when(has("down", side))(lambda: act(k_copy(slot, side, c), side))
        for side in (0, 1):
            pl.when(has("east", side))(lambda: act(i_copy(slot, side, c), side))
        for side in (0, 1):
            edge = 0 if side == 0 else pieces - 1
            pl.when(has("south", side) & (c == edge))(lambda: act(j_copy(slot, side), side))

    def send(slot, c):
        each_copy(slot, c, lambda copy, side: copy.start())

    def sent(slot, c):
        each_copy(slot, c, lambda copy, side: copy.wait_send())

    def received(slot, c):
        for side in (0, 1):
            pl.when(has("down", side))(lambda: k_copy(slot, 1 - side, c).wait_recv())
        for side in (0, 1):
            pl.when(has("east", side))(lambda: i_copy(slot, 1 - side, c).wait_recv())
        for side in (0, 1):
            edge = 0 if side == 0 else pieces - 1
            pl.when(has("south", side) & (c == edge))(
                lambda: j_copy(slot, 1 - side).wait_recv()
            )

    @pl.loop(0, pieces)
    def _(c):
        load(piece_of(c)).start()

    @pl.loop(0, pieces)
    def _(c):
        for d in range(3):
            load_flow(d, piece_of(c)).start()

    barrier = pltpu.get_barrier_semaphore()
    for axis in ("east", "down"):
        for side in (0, 1):
            @pl.when(has(axis, side))
            def _():
                pl.semaphore_signal(barrier, 1, device_id=beside(axis, side), device_id_type=MESH)
    for offset in range(1, n_south):
        other = {"south": lax.rem(south + offset, n_south)}
        pl.semaphore_signal(barrier, 1, device_id=other, device_id_type=MESH)

    for side in (0, 1):
        @pl.when(jnp.logical_not(has("down", side)))
        def _():
            @pl.loop(0, nj)
            def _(r):
                for slot in (0, 1):
                    face_in[slot, side, r] = jnp.zeros(face_in.shape[3:], jnp.float32)

        @pl.when(jnp.logical_not(has("east", side)))
        def _():
            @pl.loop(0, nj)
            def _(r):
                for slot in (0, 1):
                    cells[slot, r + 1, 0 if side == 0 else ni + 1] = jnp.zeros(
                        cells.shape[3:], jnp.float32)

        @pl.when(jnp.logical_not(has("south", side)))
        def _():
            for slot in (0, 1):
                cells[slot, 0 if side == 0 else nj + 1, pl.ds(1, ni)] = jnp.zeros(
                    field.shape[1:], jnp.float32)

    peers = n_south - 1
    for axis in ("east", "down"):
        for side in (0, 1):
            peers = peers + has(axis, side).astype(jnp.int32)
    pl.semaphore_wait(barrier, peers)

    @pl.loop(0, pieces)
    def _(index):
        c = piece_of(index)
        load(c).wait()

        @pl.loop(0, rows)
        def _(offset):
            r = c * rows + offset
            values = cells[0, r + 1, pl.ds(1, ni)]
            face_out[0, 0, r] = values[:, 0, :]
            face_out[0, 1, r] = values[:, nk - 1, :]

        send(0, c)

    height = lax.broadcasted_iota(jnp.int32, field.shape[1:], 1)

    def advanced(slot, r):
        middle = cells[slot, r + 1, pl.ds(1, ni)]
        j_low = cells[slot, r, pl.ds(1, ni)]
        j_high = cells[slot, r + 2, pl.ds(1, ni)]
        i_low = cells[slot, r + 1, pl.ds(0, ni)]
        i_high = cells[slot, r + 1, pl.ds(2, ni)]
        k_low = jnp.where(
            height == 0, face_in[slot, 0, r][:, None, :], pltpu.roll(middle, 1, 1))
        k_high = jnp.where(
            height == nk - 1, face_in[slot, 1, r][:, None, :], pltpu.roll(middle, nk - 1, 1))
        spread = (j_low + j_high) + (i_low + i_high) + (k_low + k_high) - 6.0 * middle
        drift = (flows[0, r] * (j_high - j_low) + flows[1, r] * (i_high - i_low)
                 + flows[2, r] * (k_high - k_low))
        return middle - drift + 0.05 * spread

    @pl.loop(1, steps)
    def _(step):
        now, later = lax.rem(step + 1, 2), lax.rem(step, 2)

        @pl.loop(0, pieces)
        def _(index):
            c = piece_of(index)

            @pl.when(step == 1)
            def _():
                for d in range(3):
                    load_flow(d, c).wait()

            @pl.when(step >= 2)
            def _():
                sent(later, c)

            received(now, c)

            @pl.loop(0, rows)
            def _(offset):
                r = c * rows + offset
                values = advanced(now, r)
                cells[later, r + 1, pl.ds(1, ni)] = values
                face_out[later, 0, r] = values[:, 0, :]
                face_out[later, 1, r] = values[:, nk - 1, :]

            send(later, c)

    now, later = (steps - 1) % 2, steps % 2

    def store(c):
        return pltpu.make_async_copy(
            cells.at[later, pl.ds(c * rows + 1, rows), pl.ds(1, ni)],
            end.at[pl.ds(c * rows, rows)],
            end_sem.at[c],
        )

    def finish(index, total):
        c = piece_of(index)
        sent(later, c)
        received(now, c)

        def row(offset, total):
            r = c * rows + offset
            values = advanced(now, r)
            cells[later, r + 1, pl.ds(1, ni)] = values
            return total + values

        total = lax.fori_loop(0, rows, row, total)
        store(c).start()
        return total

    zero = jnp.zeros(field.shape[1:], jnp.float32)
    mean = lax.fori_loop(0, pieces, finish, zero) * (1.0 / nj)

    def square(r, total):
        centred = cells[later, r + 1, pl.ds(1, ni)] - mean
        return total + centred * centred

    squares = lax.fori_loop(0, nj, square, zero)
    stats[south, 0] = mean
    stats[south, 1] = squares

    def stat_copy(offset, owner):
        target = lax.rem(south + offset, n_south)
        return pltpu.make_async_remote_copy(
            stats.at[owner], stats.at[owner], stat_send.at[offset - 1], stat_recv.at[offset - 1],
            device_id={"south": target}, device_id_type=MESH,
        )

    for offset in range(1, n_south):
        stat_copy(offset, south).start()

    @pl.loop(0, pieces)
    def _(c):
        sent(now, c)
        store(c).wait()

    for offset in range(1, n_south):
        owner = lax.rem(south + n_south - offset, n_south)
        stat_copy(offset, owner).wait_recv()
    whole_mean = stats[0, 0]
    for other in range(1, n_south):
        whole_mean = whole_mean + stats[other, 0]
    whole_mean = whole_mean * (1.0 / n_south)
    whole_squares = zero
    for other in range(n_south):
        away = stats[other, 0] - whole_mean
        whole_squares = whole_squares + (stats[other, 1] + nj * (away * away))
    mean_out[...] = whole_mean
    scale_out[...] = lax.rsqrt(whole_squares * (1.0 / (nj * n_south)) + 0.0001)
    for offset in range(1, n_south):
        stat_copy(offset, south).wait_send()


def scale(values, mean, factor, standardized, copied):
    block = values[...]
    copied[...] = block
    standardized[...] = (block - mean[...][None]) * factor[...][None]


def per_device(counts, field_values, flow_j, flow_i, flow_k):
    nj, ni, nk, levels = field_values.shape
    pieces = PIECES
    n_south = counts[0]
    plane = (ni, nk, levels)
    end, mean, factor = pl.pallas_call(
        functools.partial(transport, counts, pieces, STEPS),
        name="transport",
        out_shape=(
            jax.ShapeDtypeStruct(field_values.shape, jnp.float32),
            jax.ShapeDtypeStruct(plane, jnp.float32),
            jax.ShapeDtypeStruct(plane, jnp.float32),
        ),
        in_specs=[pl.BlockSpec(memory_space=pltpu.HBM)] * 4,
        out_specs=(
            pl.BlockSpec(memory_space=pl.ANY),
            pl.BlockSpec(memory_space=pltpu.VMEM),
            pl.BlockSpec(memory_space=pltpu.VMEM),
        ),
        scratch_shapes=[
            pltpu.VMEM((2, nj + 2, ni + 2, nk, levels), jnp.float32),
            pltpu.VMEM((3,) + field_values.shape, jnp.float32),
            pltpu.VMEM((2, 2, nj, ni, levels), jnp.float32),
            pltpu.VMEM((2, 2, nj, ni, levels), jnp.float32),
            pltpu.VMEM((n_south, 2) + plane, jnp.float32),
            pltpu.SemaphoreType.DMA((pieces,)),
            pltpu.SemaphoreType.DMA((3, pieces)),
            pltpu.SemaphoreType.DMA((pieces,)),
            pltpu.SemaphoreType.DMA((2, 2, pieces)),
            pltpu.SemaphoreType.DMA((2, 2, pieces)),
            pltpu.SemaphoreType.DMA((2, 2, pieces)),
            pltpu.SemaphoreType.DMA((2, 2, pieces)),
            pltpu.SemaphoreType.DMA((2, 2)),
            pltpu.SemaphoreType.DMA((2, 2)),
            pltpu.SemaphoreType.DMA((max(n_south - 1, 1),)),
            pltpu.SemaphoreType.DMA((max(n_south - 1, 1),)),
        ],
        compiler_params=pltpu.CompilerParams(
            collective_id=0, has_side_effects=True, vmem_limit_bytes=34 * 2**20
        ),
    )(*(pltpu.with_memory_space_constraint(array, pltpu.HBM)
        for array in (field_values, flow_j, flow_i, flow_k)))
    rows = nj // pieces
    block = pl.BlockSpec((rows,) + plane, lambda c: (c, 0, 0, 0))
    flat = pl.BlockSpec(plane, lambda c: (0, 0, 0))
    return pl.pallas_call(
        scale,
        name="scale",
        grid=(nj // rows,),
        in_specs=[block, flat, flat],
        out_specs=(block, block),
        out_shape=(jax.ShapeDtypeStruct(field_values.shape, jnp.float32),) * 2,
        compiler_params=pltpu.CompilerParams(vmem_limit_bytes=16 * 2**20),
    )(end, mean, factor)


def solution(mesh):
    counts = tuple(mesh.shape[axis] for axis in ("south", "east", "down"))
    spec = P("south", "east", "down", None)
    return jax.shard_map(
        functools.partial(per_device, counts),
        mesh=mesh,
        in_specs=(spec,) * 4,
        out_specs=(spec, spec),
        check_vma=False,
    )
```

time: 321 us -> 85.5 us (0.27); the launches traced: 316 us -> 85.3 us
  starting transfers between devices: 105 us -> 0 us
  waiting for transfers between devices: 98.2 us -> 0 us
  Pallas kernels: 0 us -> 84.7 us
  other arithmetic: 83.1 us -> 0 us
  blocking collectives: 15.8 us -> 0 us
  local copies, waits for them, and re-layouts: 12.4 us -> 0 us
    ppermute x36 -> x0, starting transfers between devices: 105 us -> none  [the longest x18 80.9 us: extended(): lax.ppermute(lax.slice_in_dim(block, block.shape[dim] - width, None, axis...]
    ppermute x36 -> x0, waiting for transfers between devices: 98.2 us -> none  [the longest x18 82.1 us: extended(): lax.ppermute(lax.slice_in_dim(block, 0, width, axis=dim), axis, backward)]
    pallas_call x0 -> x2, Pallas kernels: none -> 84.7 us  [the longest x1 80.2 us: per_device(): pl.pallas_call(functools.partial(transport, counts, pieces, STEPS), name=...]
    add x5 -> x0, other arithmetic: 54.7 us -> none  [advance(): middle - flow_j * slopes[0] - flow_i * slopes[1] - flow_k * slopes[2]]
    psum x2 -> x0, blocking collectives: 15.8 us -> none  [the longest x1 8.94 us: per_device(): lax.psum(jnp.sum(centred * centred, axis=0, keepdims=True), 'south') / count]
    reduce_sum x2 -> x0, other arithmetic: 13.7 us -> none  [the longest x1 11 us: per_device(): jnp.sum(field_values, axis=0, keepdims=True)]
    ppermute x12 -> x0, local copies, waits for them, and re-layouts: 8.22 us -> none  [the longest x6 4.11 us: extended(): lax.ppermute(lax.slice_in_dim(block, 0, width, axis=dim), axis, backward)]
    concatenate x10 -> x0, other arithmetic: 8.01 us -> none  [extended(): block = jnp.concatenate([low, block, high], axis=dim)]
  transfers between devices with their start and end apart: 36 -> 0, of which waited for: 34 -> 0; matrix products, arithmetic and copies ran while one was open for 2% -> 0% of each run, Pallas kernels for 0% -> 0%
where the time goes in v1:
time: 85.5 us; the launch traced here: 85.3 us
  Pallas kernels  84.7 us (99%)
    pallas_call x1, Pallas kernels, per_device(): pl.pallas_call(functools.partial(transport, counts, pieces, STEPS), name=...  80.2 us
    pallas_call x1, Pallas kernels, per_device(): pl.pallas_call(scale, name='scale', grid=(nj // rows,), in_specs=[block,...  4.45 us

profile of v1, /device:TPU:0, one launch (start us, length us, event | category | flops | bytes accessed | tf_op | source)
XLA Modules:
  0.0 85.3 jit_solution(17121683193760957189)
XLA Ops:
  0.6 80.2 %transport.1 = (f32[128,8,8,128]{3,2,1,0:T(8,128)S(1)}, f32[8,8,128]{2,1,0:T(8,128)S(1)}, f32[8,8,128]{2,1,0:T(8,128)S(1)}) custom-call(f32[128,8,8,128]{3,2,1,0:T(8,128)} %field.1, f32[128,8,8,128]{3,2,1,0:T(8,128)} %flow_j.1, f32[128,8,8,128]{3,2,1,0:T(8,128)} %flow_i.1, f32[128,8,8,128]{3,2,1,0:T(8,128)} %flow_k.1), custom_call_target="tpu_custom_call" | custom-call | tf_op jit(solution)/shard_map/transport/pallas_call | solution.py:285
  80.9 4.4 %scale.1 = (f32[128,8,8,128]{3,2,1,0:T(8,128)}, f32[128,8,8,128]{3,2,1,0:T(8,128)}) custom-call(f32[128,8,8,128]{3,2,1,0:T(8,128)S(1)} %get-tuple-element.5.values, f32[8,8,128]{2,1,0:T(8,128)S(1)} %get-tuple-element.6.mean, f32[8,8,128]{2,1,0:T(8,128)S(1)} %get-tuple-element.7.factor), custom_call_target="tpu_custom_call" | custom-call | tf_op jit(solution)/shard_map/scale/pallas_call | solution.py:325

commit v2 on v1

--- a/solution.py
+++ b/solution.py
@@ -13,7 +13,7 @@
 
 
 def transport(counts, pieces, steps, field, flow_j, flow_i, flow_k, end, mean_out, scale_out,
-              cells, flows, face_out, face_in, stats,
+              cells, flows, face_out, face_in, stats, means,
               load_sem, flow_sem, end_sem, k_send, k_recv, i_send, i_recv, j_send, j_recv,
               stat_send, stat_recv):
     n_south, n_east, n_down = counts
@@ -97,15 +97,6 @@
                 lambda: j_copy(slot, 1 - side).wait_recv()
             )
 
-    @pl.loop(0, pieces)
-    def _(c):
-        load(piece_of(c)).start()
-
-    @pl.loop(0, pieces)
-    def _(c):
-        for d in range(3):
-            load_flow(d, piece_of(c)).start()
-
     barrier = pltpu.get_barrier_semaphore()
     for axis in ("east", "down"):
         for side in (0, 1):
@@ -115,6 +106,32 @@
     for offset in range(1, n_south):
         other = {"south": lax.rem(south + offset, n_south)}
         pl.semaphore_signal(barrier, 1, device_id=other, device_id_type=MESH)
+
+    @pl.loop(0, pieces)
+    def _(c):
+        load(piece_of(c)).start()
+
+    peers = n_south - 1
+    for axis in ("east", "down"):
+        for side in (0, 1):
+            peers = peers + has(axis, side).astype(jnp.int32)
+    pl.semaphore_wait(barrier, peers)
+
+    @pl.loop(0, pieces)
+    def _(index):
+        c = piece_of(index)
+        load(c).wait()
+
+        @pl.loop(0, rows)
+        def _(offset):
+            r = c * rows + offset
+            values = cells[0, r + 1, pl.ds(1, ni)]
+            face_out[0, 0, r] = values[:, 0, :]
+            face_out[0, 1, r] = values[:, nk - 1, :]
+
+        send(0, c)
+        for d in range(3):
+            load_flow(d, c).start()
 
     for side in (0, 1):
         @pl.when(jnp.logical_not(has("down", side)))
@@ -137,26 +154,6 @@
             for slot in (0, 1):
                 cells[slot, 0 if side == 0 else nj + 1, pl.ds(1, ni)] = jnp.zeros(
                     field.shape[1:], jnp.float32)
-
-    peers = n_south - 1
-    for axis in ("east", "down"):
-        for side in (0, 1):
-            peers = peers + has(axis, side).astype(jnp.int32)
-    pl.semaphore_wait(barrier, peers)
-
-    @pl.loop(0, pieces)
-    def _(index):
-        c = piece_of(index)
-        load(c).wait()
-
-        @pl.loop(0, rows)
-        def _(offset):
-            r = c * rows + offset
-            values = cells[0, r + 1, pl.ds(1, ni)]
-            face_out[0, 0, r] = values[:, 0, :]
-            face_out[0, 1, r] = values[:, nk - 1, :]
-
-        send(0, c)
 
     height = lax.broadcasted_iota(jnp.int32, field.shape[1:], 1)
 
@@ -213,7 +210,7 @@
             end_sem.at[c],
         )
 
-    def finish(index, total):
+    def finish(index, squares):
         c = piece_of(index)
         sent(later, c)
         received(now, c)
@@ -224,18 +221,25 @@
             cells[later, r + 1, pl.ds(1, ni)] = values
             return total + values
 
-        total = lax.fori_loop(0, rows, row, total)
+        own_mean = lax.fori_loop(0, rows, row, zero) * (1.0 / rows)
         store(c).start()
-        return total
+        means[index] = own_mean
+
+        def square(offset, total):
+            centred = cells[later, c * rows + offset + 1, pl.ds(1, ni)] - own_mean
+            return total + centred * centred
+
+        return lax.fori_loop(0, rows, square, squares)
 
     zero = jnp.zeros(field.shape[1:], jnp.float32)
-    mean = lax.fori_loop(0, pieces, finish, zero) * (1.0 / nj)
-
-    def square(r, total):
-        centred = cells[later, r + 1, pl.ds(1, ni)] - mean
-        return total + centred * centred
-
-    squares = lax.fori_loop(0, nj, square, zero)
+    squares = lax.fori_loop(0, pieces, finish, zero)
+    mean = means[0]
+    for index in range(1, pieces):
+        mean = mean + means[index]
+    mean = mean * (1.0 / pieces)
+    for index in range(pieces):
+        away = means[index] - mean
+        squares = squares + rows * (away * away)
     stats[south, 0] = mean
     stats[south, 1] = squares
 
@@ -302,6 +306,7 @@
             pltpu.VMEM((2, 2, nj, ni, levels), jnp.float32),
             pltpu.VMEM((2, 2, nj, ni, levels), jnp.float32),
             pltpu.VMEM((n_south, 2) + plane, jnp.float32),
+            pltpu.VMEM((pieces,) + plane, jnp.float32),
             pltpu.SemaphoreType.DMA((pieces,)),
             pltpu.SemaphoreType.DMA((3, pieces)),
             pltpu.SemaphoreType.DMA((pieces,)),

time: 85.5 us -> 84.7 us (level)
  no operation moved by 1% of the time
where the time goes in v2:
time: 84.7 us; the launch traced here: 84.5 us
  Pallas kernels  83.9 us (99%)
    pallas_call x1, Pallas kernels, per_device(): pl.pallas_call(functools.partial(transport, counts, pieces, STEPS), name=...  79.4 us
    pallas_call x1, Pallas kernels, per_device(): pl.pallas_call(scale, name='scale', grid=(nj // rows,), in_specs=[block,...  4.45 us

profile of v2, /device:TPU:0, one launch (start us, length us, event | category | flops | bytes accessed | tf_op | source)
XLA Modules:
  0.0 84.5 jit_solution(14126975620119508962)
XLA Ops:
  0.6 79.4 %transport.1 = (f32[128,8,8,128]{3,2,1,0:T(8,128)S(1)}, f32[8,8,128]{2,1,0:T(8,128)S(1)}, f32[8,8,128]{2,1,0:T(8,128)S(1)}) custom-call(f32[128,8,8,128]{3,2,1,0:T(8,128)} %field.1, f32[128,8,8,128]{3,2,1,0:T(8,128)} %flow_j.1, f32[128,8,8,128]{3,2,1,0:T(8,128)} %flow_i.1, f32[128,8,8,128]{3,2,1,0:T(8,128)} %flow_k.1), custom_call_target="tpu_custom_call" | custom-call | tf_op jit(solution)/shard_map/transport/pallas_call | solution.py:289
  80.0 4.4 %scale.1 = (f32[128,8,8,128]{3,2,1,0:T(8,128)}, f32[128,8,8,128]{3,2,1,0:T(8,128)}) custom-call(f32[128,8,8,128]{3,2,1,0:T(8,128)S(1)} %get-tuple-element.5.values, f32[8,8,128]{2,1,0:T(8,128)S(1)} %get-tuple-element.6.mean, f32[8,8,128]{2,1,0:T(8,128)S(1)} %get-tuple-element.7.factor), custom_call_target="tpu_custom_call" | custom-call | tf_op jit(solution)/shard_map/scale/pallas_call | solution.py:330
